TPU v7x, 32 devices: a whole 2x2x4 slice. The times are simulated.
32 devices in a mesh: mem: 4 (over y, x), tile: 8 (over z, core).
Axes of the slice: x: 2, y: 2, z: 4, core: 2. Of those that a mesh axis runs over, the one named last changes fastest.
Arguments:
- ensemble: bfloat16 [8, 256, 64, 256], P('mem', None, 'tile'), may hold values from -4 to 4
- control: float32 [8, 64, 256], P('mem', 'tile'), may hold values from -6 to 6
- weights: float32 [8], P('mem'), may hold values from 0.1 to 0.6
- member_band: int32 [8], P('mem'), may hold values from 0 to 3
- spread: float32 [4], replicated, may hold values from 0.05 to 0.24
- advect: float32 [2, 256], replicated, may hold values from -0.9 to 0.9
- damping: float32 [256], replicated, may hold values from 0.02 to 0.2
- innovation: float32 [256, 64, 256], P(None, 'tile'), may hold values from -4 to 4
- obs_weight: float32 [64, 256], P('tile'), may hold values from 0.3 to 27
Outputs:
- grad_control: float32 [8, 64, 256], P('mem', 'tile')
- grad_weight: float32 [8], P('mem')
All inputs are finite; a program needn't handle non-finite values.
Results may differ from a plain program's by a relative error of at most 0.0003.
Values sent between devices are 32-bit elements; how exact they have to be, the bound alone decides.
A program may use at most 64 MiB of HBM per device.

v0:
```python
import functools
import math

import jax
import jax.numpy as jnp
from jax import lax
from jax.experimental import pallas as pl
from jax.experimental.pallas import tpu as pltpu
from jax.sharding import PartitionSpec as P

SWEEPS = 8
CHUNKS = 4
SHIPPED = 1
LANES = 128
MESH = pl.DeviceIdType.MESH


def factors(n):
    a = max(d for d in range(1, n + 1) if n % d == 0 and d * d <= n)
    return a, n // a


def y_pair(f):
    ny = f.shape[-1]
    col = lax.broadcasted_iota(jnp.int32, f.shape, 1)
    north = jnp.where(col == ny - 1, 0.0, pltpu.roll(f, ny - 1, 1))
    south = jnp.where(col == 0, 0.0, pltpu.roll(f, 1, 1))
    return north, south


def sweeps(f, rates):
    rows = f.shape[0]
    for _ in range(SWEEPS):
        north, south = y_pair(f)
        east = pltpu.roll(f, rows - 1, 0)
        west = pltpu.roll(f, 1, 0)
        f = f + rates * (east + west + north + south - 4.0 * f)
    return f


def kernel(
    n, tiles, steps, ship,
    ens, control_h, weights_h, band_h, spread_h, advect_h, damping_h, innov, obs_h,
    out_h, gw_h,
    args, outs, local_sems,
    e_v, fields, per_q,
    sems,
):
    a, b = factors(n)
    control, weights, band, spread, advect, damping, obs = args
    out, gw_out = outs
    arg_sem, out_sem, e_sem, i_sem = local_sems
    loc, scl, proj, ch, wh, wb, ph, gwr = fields
    ml, rows, ny = control.shape
    vl = ens.shape[1]
    nc = ny // LANES
    me = lax.axis_index("mem")
    t = lax.axis_index("tile")
    nxt = (t + 1) % tiles
    prv = (t + tiles - 1) % tiles
    ia = me // b
    ib = me % b
    first = (b, a)
    second = (a, b)
    fi = (ib, ia)
    gi = (ia, ib)
    size = [vl // (2 * f) for f in first]
    chunk = [k // steps for k in size]
    lone = tuple(range(ship, steps))
    sent = tuple(range(ship))

    def device(q, f, g):
        return g * b + f if q == 0 else f * b + g

    def start_of(q, owner, s):
        return pl.multiple_of(q * (vl // 2) + (owner * steps + s) * chunk[q], chunk[q])

    def ahead(q, d):
        return (fi[q] + d) % first[q]

    def behind(q, d):
        return (fi[q] + first[q] - d) % first[q]

    def to_first(q, d):
        return device(q, ahead(q, d), gi[q])

    def back_first(q, d):
        return device(q, behind(q, d), gi[q])

    def to_second(q, d):
        return device(q, fi[q], (gi[q] + d) % second[q])

    def remote(kind, index, src, dst, axis, dev):
        s_sem, r_sem = sems[kind]
        return pltpu.make_async_remote_copy(
            src_ref=src, dst_ref=dst, send_sem=s_sem.at[index], recv_sem=r_sem.at[index],
            device_id={axis: dev}, device_id_type=MESH,
        )

    def lanes(c):
        return slice(c * LANES, (c + 1) * LANES)

    barrier = pltpu.get_barrier_semaphore()
    for d in range(1, tiles):
        pl.semaphore_signal(
            barrier, inc=1, device_id={"tile": (t + d) % tiles}, device_id_type=MESH
        )
    for q in range(2):
        for d in range(1, first[q]):
            pl.semaphore_signal(
                barrier, inc=1, device_id={"mem": to_first(q, d)}, device_id_type=MESH
            )

    def ens_copy(q, d, late):
        if d == 0:
            where = pl.ds(start_of(q, fi[q], 0), size[q])
        elif late:
            where = pl.ds(start_of(q, ahead(q, d), ship), (steps - ship) * chunk[q])
        else:
            where = pl.ds(start_of(q, ahead(q, d), 0), ship * chunk[q])
        return pltpu.make_async_copy(
            ens.at[:, where], e_v.at[:, where], e_sem.at[q, d, int(late)]
        )

    arg_copy = [
        pltpu.make_async_copy(src, dst, arg_sem.at[i])
        for i, (src, dst) in enumerate((
            (control_h, control), (obs_h, obs), (weights_h, weights), (band_h, band),
            (spread_h, spread), (advect_h, advect), (damping_h, damping),
        ))
    ]
    innov_copy = [
        pltpu.make_async_copy(
            innov.at[pl.ds(start_of(q, fi[q], 0), size[q]), :, lanes(c)],
            per_q["iv"][q].at[:, c],
            i_sem.at[q, c],
        )
        for q in range(2)
        for c in range(nc)
    ]
    early = [ens_copy(q, d, False) for q in range(2) for d in range(1, first[q])]
    late = [ens_copy(q, 0, False) for q in range(2)]
    late += [ens_copy(q, d, True) for q in range(2) for d in range(1, first[q])]
    for c in early + arg_copy + late + innov_copy:
        c.start()

    def ship_copy(q, i, d):
        return remote(
            "ship", (q, i, d - 1), per_q["es"][q].at[i, d - 1], per_q["er"][q].at[i, d - 1],
            "mem", to_first(q, d),
        )

    def scl_copy(q, d):
        return remote(
            "scl", (q, d - 1), scl, per_q["sr"][q].at[d - 1], "mem", to_first(q, d)
        )

    def part_copy(q, s, d):
        i = s - ship
        return remote(
            "part", (q, i, d - 1), per_q["to"][q].at[i, d - 1], per_q["r1"][q].at[i, d - 1],
            "mem", to_first(q, d),
        )

    def swap_copy(q, s, d):
        return remote(
            "swap", (q, s, d - 1),
            per_q["part"][q].at[pl.ds(s * chunk[q], chunk[q])], per_q["r2"][q].at[s, d - 1],
            "mem", to_second(q, d),
        )

    def grad_copy(q, s, d):
        i = s - ship
        return remote(
            "grad", (q, i, d - 1),
            per_q["grad"][q].at[pl.ds(s * chunk[q], chunk[q])], per_q["gr"][q].at[i, d - 1],
            "mem", to_first(q, d),
        )

    def proj_copy(q, d):
        return remote(
            "proj", (q, d - 1), per_q["pp"][q].at[d - 1], per_q["pr"][q].at[d - 1],
            "mem", back_first(q, d),
        )

    def both(kind, k, src, dst):
        return (
            remote(kind, k, src, dst.at[0], "tile", nxt),
            remote(kind, k + 1, src, dst.at[1], "tile", prv),
        )

    def innov_halo(q):
        ov = per_q["ov"][q]
        return (
            remote("edge", 4 + 2 * q, ov.at[rows], ov.at[0], "tile", nxt),
            remote("edge", 5 + 2 * q, ov.at[1], ov.at[rows + 1], "tile", prv),
        )

    def halo(q, s):
        ip = per_q["ip"][q]
        where = pl.ds(s * chunk[q], chunk[q])
        return (
            remote("halo", (0, q, s), ip.at[pl.ds(rows, 2), where], ip.at[pl.ds(0, 2), where], "tile", nxt),
            remote("halo", (1, q, s), ip.at[pl.ds(2, 2), where], ip.at[pl.ds(rows + 2, 2), where], "tile", prv),
        )

    c_copy = both("edge", 0, control, ch)
    w_copy = both("edge", 2, obs, wh)
    p_copy = both("edge", 8, scl, ph)
    o_copy = innov_halo(0) + innov_halo(1)

    for c in early:
        c.wait()
    for q in range(2):
        for i in sent:
            for d in range(1, first[q]):
                where = pl.ds(start_of(q, ahead(q, d), i), chunk[q])
                for m in range(ml):
                    e = e_v[m, where].astype(jnp.float32)
                    for c in range(nc):
                        per_q["es"][q][i, d - 1, m, :, c] = e[:, :, lanes(c)]
    for c in arg_copy[:2]:
        c.wait()
    pl.semaphore_wait(barrier, tiles - 1 + a - 1 + b - 1)
    for c in c_copy + w_copy:
        c.start()
    for i in sent:
        for q in range(2):
            for d in range(1, first[q]):
                ship_copy(q, i, d).start()

    for c in innov_copy:
        c.wait()
    for q in range(2):
        flat = per_q["iv"][q].reshape(size[q] * nc * rows, LANES)
        ov = per_q["ov"][q]

        @pl.loop(0, size[q] // 8)
        def _(j):
            for c in range(nc):
                for r in range(rows):
                    ov[1 + r, pl.ds(pl.multiple_of(j * 8, 8), 8), lanes(c)] = flat[
                        pl.ds(j * (8 * nc * rows) + c * rows + r, 8, stride=nc * rows), :
                    ]

    for c in o_copy:
        c.start()
    for c in arg_copy[2:]:
        c.wait()
    for q in range(2):
        coef = per_q["coef"][q]
        base = start_of(q, fi[q], 0)
        sub = lax.broadcasted_iota(jnp.int32, (8, LANES), 0)

        @pl.loop(0, size[q] // 8)
        def _(j):
            for kind, value in enumerate((
                lambda k: advect[0, k], lambda k: advect[1, k], lambda k: damping[k]
            )):
                v = jnp.full((8, LANES), value(base + j * 8), jnp.float32)
                for i in range(1, 8):
                    v = jnp.where(sub == i, value(base + j * 8 + i), v)
                coef[kind, pl.ds(pl.multiple_of(j * 8, 8), 8)] = v

    rates = jnp.concatenate(
        [jnp.full((3 * rows, ny), spread[band[m]], jnp.float32) for m in range(ml)], axis=0
    )
    for c in c_copy:
        c.wait_recv()
    field = []
    for m in range(ml):
        field += [ch[0, m], control[m], ch[1, m]]
    field = sweeps(jnp.concatenate(field, axis=0), rates)
    for m in range(ml):
        center = field[(3 * m + 1) * rows : (3 * m + 2) * rows]
        loc[m] = center
        scl[m] = weights[m] * center
        proj[m] = jnp.zeros_like(center)
        for q in range(2):
            for d in range(1, first[q]):
                per_q["pp"][q][d - 1, m] = jnp.zeros_like(center)
    for q in range(2):
        for d in range(1, first[q]):
            if ship:
                scl_copy(q, d).start()
    for c in late:
        c.wait()

    def own_sum(q, owner, s, c):
        where = pl.ds(start_of(q, owner, s), chunk[q])
        total = None
        for m in range(ml):
            term = e_v[m, where, :, lanes(c)].astype(jnp.float32) * scl[m, :, lanes(c)][None]
            total = term if total is None else total + term
        return total

    for s in lone:
        for q in range(2):
            for d in range(1, first[q]):
                for c in range(nc):
                    per_q["to"][q][s - ship, d - 1, :, c] = own_sum(q, ahead(q, d), s, c)
                part_copy(q, s, d).start()
    for s in range(steps):
        for q in range(2):
            for c in range(nc):
                per_q["part"][q][s * chunk[q] : (s + 1) * chunk[q], c] = own_sum(q, fi[q], s, c)
    for c in w_copy:
        c.wait_recv()
    weight = (wh[0, rows - 1 :], obs[...], wh[1, :1])
    wb[0] = jnp.broadcast_to(weight[0], (8, ny))
    wb[rows + 1] = jnp.broadcast_to(weight[2], (8, ny))
    for r in range(rows):
        wb[1 + r] = jnp.broadcast_to(weight[1][r : r + 1], (8, ny))

    def add_first(s):
        for q in range(2):
            where = slice(s * chunk[q], (s + 1) * chunk[q])
            for c in range(nc):
                total = per_q["part"][q][where, c]
                for d in range(1, first[q]):
                    if s >= ship:
                        if c == 0:
                            part_copy(q, s, d).wait_recv()
                        total = total + per_q["r1"][q][s - ship, d - 1, :, c]
                    else:
                        if c == 0:
                            ship_copy(q, s, d).wait_recv()
                            if s == 0:
                                scl_copy(q, d).wait_recv()
                        for m in range(ml):
                            total = total + (
                                per_q["er"][q][s, d - 1, m, :, c]
                                * per_q["sr"][q][d - 1, m, :, lanes(c)][None]
                            )
                per_q["part"][q][where, c] = total
            for d in range(1, second[q]):
                swap_copy(q, s, d).start()

    def add_second(s):
        for q in range(2):
            for d in range(1, second[q]):
                swap_copy(q, s, d).wait_recv()
            flat = per_q["part"][q].reshape(size[q] * nc * rows, LANES)
            peers = [
                per_q["r2"][q].at[s, d - 1].reshape(chunk[q] * nc * rows, LANES)
                for d in range(1, second[q])
            ]
            ip = per_q["ip"][q]

            @pl.loop(0, chunk[q] // 8)
            def _(j):
                for c in range(nc):
                    for r in range(rows):
                        at = j * (8 * nc * rows) + c * rows + r
                        total = flat[
                            pl.ds(s * (chunk[q] * nc * rows) + at, 8, stride=nc * rows), :
                        ]
                        for p in peers:
                            total = total + p[pl.ds(at, 8, stride=nc * rows), :]
                        ip[2 + r, pl.ds(pl.multiple_of(s * chunk[q] + j * 8, 8), 8), lanes(c)] = total

            for c in halo(q, s):
                c.start()

    def adjoint(s):
        col = lax.broadcasted_iota(jnp.int32, (8, ny), 1)
        for q in range(2):
            for c in halo(q, s):
                c.wait_recv()
            flat = per_q["grad"][q].reshape(size[q] * nc * rows, LANES)
            ip = per_q["ip"][q]
            ov = per_q["ov"][q]
            coef = per_q["coef"][q]

            @pl.loop(0, chunk[q] // 8)
            def _(j):
                where = pl.ds(pl.multiple_of(s * chunk[q] + j * 8, 8), 8)
                ax, ay, e = (
                    jnp.concatenate([coef[k, where]] * nc, axis=1) for k in range(3)
                )
                mid = 1.0 - 4.0 * e
                up = e - 0.5 * ax
                down = e + 0.5 * ax
                left = e - 0.5 * ay
                right = e + 0.5 * ay
                north1 = jnp.where(col == ny - 1, 0.0, left)
                south1 = jnp.where(col == 0, 0.0, right)
                north2 = jnp.where(col == ny - 1, 0.0, right)
                south2 = jnp.where(col == 0, 0.0, left)

                def turn(f):
                    return pltpu.roll(f, ny - 1, 1), pltpu.roll(f, 1, 1)

                f = [ip[r, where, :] for r in range(rows + 4)]
                w = []
                for r in range(1, rows + 3):
                    north, south = turn(f[r])
                    d = (
                        mid * f[r] + up * f[r + 1] + down * f[r - 1]
                        + north1 * north + south1 * south
                    )
                    w.append(wb[r - 1] * (d - ov[r - 1, where, :]))
                for r in range(1, rows + 1):
                    north, south = turn(w[r])
                    g = (
                        mid * w[r] + down * w[r + 1] + up * w[r - 1]
                        + north2 * north + south2 * south
                    )
                    for c in range(nc):
                        at = (s * chunk[q] + j * 8) * (nc * rows) + c * rows + r - 1
                        flat[pl.ds(at, 8, stride=nc * rows), :] = g[:, lanes(c)]

            if s >= ship:
                for d in range(1, first[q]):
                    grad_copy(q, s, d).start()

    def project_own(s):
        for q in range(2):
            where = pl.ds(start_of(q, fi[q], s), chunk[q])
            for c in range(nc):
                g = per_q["grad"][q][s * chunk[q] : (s + 1) * chunk[q], c]
                for m in range(ml):
                    e = e_v[m, where, :, lanes(c)].astype(jnp.float32)
                    proj[m, :, lanes(c)] += jnp.sum(e * g, axis=0)
                if s < ship:
                    for d in range(1, first[q]):
                        for m in range(ml):
                            e = per_q["er"][q][s, d - 1, m, :, c]
                            per_q["pp"][q][d - 1, m, :, lanes(c)] += jnp.sum(e * g, axis=0)

    def project_in(s):
        for q in range(2):
            for d in range(1, first[q]):
                grad_copy(q, s, d).wait_recv()
                where = pl.ds(start_of(q, behind(q, d), s), chunk[q])
                for c in range(nc):
                    g = per_q["gr"][q][s - ship, d - 1, :, c]
                    for m in range(ml):
                        e = e_v[m, where, :, lanes(c)].astype(jnp.float32)
                        proj[m, :, lanes(c)] += jnp.sum(e * g, axis=0)

    order = lone + sent
    scope = jax.named_scope
    for s in order:
        with scope(f"add_first{s}"):
            add_first(s)
    lag = 1
    for tick in range(len(order) + lag):
        if tick < len(order):
            with scope(f"add_second{order[tick]}"):
                add_second(order[tick])
        if tick == lag:
            for c in o_copy:
                c.wait_recv()
        if tick >= lag:
            s = order[tick - lag]
            with scope(f"adjoint{s}"):
                adjoint(s)
            with scope(f"project_own{s}"):
                project_own(s)
    if ship:
        for q in range(2):
            for d in range(1, first[q]):
                proj_copy(q, d).start()
    for s in lone:
        with scope(f"project_in{s}"):
            project_in(s)
    with scope("tail"):
        if ship:
            for q in range(2):
                for d in range(1, first[q]):
                    proj_copy(q, d).wait_recv()
        for m in range(ml):
            total = proj[m]
            if ship:
                for q in range(2):
                    for d in range(1, first[q]):
                        total = total + per_q["pr"][q][d - 1, m]
                        scl_copy(q, d).wait_send() if m == 0 else None
            proj[m] = total
            scl[m] = weights[m] * total
    with scope("halo_out"):
        for c in p_copy:
            c.start()
        row = lax.broadcasted_iota(jnp.int32, (8, LANES), 0)
        sums = jnp.zeros((8, LANES), jnp.float32)
        for m in range(ml):
            v = jnp.sum(loc[m] * proj[m], axis=0, keepdims=True)
            v = sum(v[:, lanes(c)] for c in range(nc))
            sums = jnp.where(row == m, jnp.broadcast_to(v, (8, LANES)), sums)
        gwr[t] = sums

        def gw_copy(d, incoming=False):
            slot = (t + tiles - d) % tiles if incoming else t
            return remote("gw", d - 1, gwr.at[slot], gwr.at[slot], "tile", (t + d) % tiles)

        for d in range(1, tiles):
            gw_copy(d).start()
        for c in p_copy:
            c.wait_recv()
    with scope("sweeps"):
        field = []
        for m in range(ml):
            field += [ph[0, m], scl[m], ph[1, m]]
        field = sweeps(jnp.concatenate(field, axis=0), rates)
        for m in range(ml):
            out[m] = control[m] + field[(3 * m + 1) * rows : (3 * m + 2) * rows]
    with scope("finish"):
        done = (
            pltpu.make_async_copy(out, out_h, out_sem.at[0]),
            pltpu.make_async_copy(gw_out, gw_h, out_sem.at[1]),
        )
        done[0].start()
        for d in range(1, tiles):
            gw_copy(d, True).wait_recv()
        total = gwr[0]
        for d in range(1, tiles):
            total = total + gwr[d]
        gw_out[...] = jnp.broadcast_to(jnp.sum(total, axis=1, keepdims=True), (8, LANES))
        done[1].start()

        for c in c_copy + w_copy + o_copy + p_copy:
            c.wait_send()
        for d in range(1, tiles):
            gw_copy(d).wait_send()
        for q in range(2):
            for s in range(steps):
                for c in halo(q, s):
                    c.wait_send()
                for d in range(1, second[q]):
                    swap_copy(q, s, d).wait_send()
                for d in range(1, first[q]):
                    if s >= ship:
                        part_copy(q, s, d).wait_send()
                        grad_copy(q, s, d).wait_send()
                    else:
                        ship_copy(q, s, d).wait_send()
            if ship:
                for d in range(1, first[q]):
                    proj_copy(q, d).wait_send()
        for c in done:
            c.wait()


def per_device(
    n, tiles,
    ensemble, control, weights, member_band, spread, advect, damping, innovation, obs_weight
):
    ml, vl, rows, ny = ensemble.shape
    a, b = factors(n)
    first, second = (b, a), (a, b)
    assert rows == SWEEPS and ny % LANES == 0 and ml <= 8 and vl % (16 * b) == 0
    nc = ny // LANES
    size = [vl // (2 * f) for f in first]
    steps = max(d for d in range(1, CHUNKS + 1) if all(k % (8 * d) == 0 for k in size))
    ship = min(SHIPPED, steps - 1)
    chunk = [k // steps for k in size]
    f32 = jnp.float32
    peers = max(a, b, 2) - 1
    dma = pltpu.SemaphoreType.DMA
    hbm = pl.BlockSpec(memory_space=pl.ANY)
    field = (rows, ny)
    tile = (nc, rows, LANES)
    vmem = lambda *shape: pltpu.VMEM(shape, f32)
    fp = [max(f - 1, 1) for f in first]
    gp = [max(g - 1, 1) for g in second]
    ns, nl = max(ship, 1), max(steps - ship, 1)

    def per(shape):
        return tuple(vmem(*shape(q)) for q in range(2))

    per_q = {
        "es": per(lambda q: (ns, fp[q], ml, chunk[q]) + tile),
        "er": per(lambda q: (ns, fp[q], ml, chunk[q]) + tile),
        "to": per(lambda q: (nl, fp[q], chunk[q]) + tile),
        "r1": per(lambda q: (nl, fp[q], chunk[q]) + tile),
        "part": per(lambda q: (size[q],) + tile),
        "r2": per(lambda q: (steps, gp[q], chunk[q]) + tile),
        "grad": per(lambda q: (size[q],) + tile),
        "gr": per(lambda q: (nl, fp[q], chunk[q]) + tile),
        "iv": per(lambda q: (size[q],) + tile),
        "ip": per(lambda q: (rows + 4, size[q], ny)),
        "ov": per(lambda q: (rows + 2, size[q], ny)),
        "coef": per(lambda q: (3, size[q], LANES)),
        "pp": per(lambda q: (fp[q], ml) + field),
        "pr": per(lambda q: (fp[q], ml) + field),
        "sr": per(lambda q: (fp[q], ml) + field),
    }
    pair = lambda *shape: (dma(shape), dma(shape))
    sems = {
        "ship": pair(2, ns, peers),
        "scl": pair(2, peers),
        "part": pair(2, nl, peers),
        "swap": pair(2, steps, peers),
        "grad": pair(2, nl, peers),
        "proj": pair(2, peers),
        "edge": pair(10),
        "halo": pair(2, 2, steps),
        "gw": pair(max(tiles - 1, 1)),
    }
    args = (
        vmem(*control.shape),
        pltpu.SMEM(weights.shape, f32),
        pltpu.SMEM(member_band.shape, member_band.dtype),
        pltpu.SMEM(spread.shape, f32),
        pltpu.SMEM(advect.shape, f32),
        pltpu.SMEM(damping.shape, f32),
        vmem(*obs_weight.shape),
    )
    fields = (
        vmem(ml, *field), vmem(ml, *field), vmem(ml, *field),
        vmem(2, ml, *field), vmem(2, *field), vmem(rows + 2, 8, ny),
        vmem(2, ml, *field), vmem(tiles, 8, LANES),
    )
    out, gw = pl.pallas_call(
        functools.partial(kernel, n, tiles, steps, ship),
        out_shape=(
            jax.ShapeDtypeStruct((ml, rows, ny), f32),
            jax.ShapeDtypeStruct((8, LANES), f32),
        ),
        in_specs=[hbm] * 9,
        out_specs=(hbm, hbm),
        scratch_shapes=[
            args,
            (vmem(*control.shape), vmem(8, LANES)),
            (dma((7,)), dma((2,)), dma((2, peers + 1, 2)), dma((2, nc))),
            pltpu.VMEM((ml, vl) + field, ensemble.dtype),
            fields,
            per_q,
            sems,
        ],
        compiler_params=pltpu.CompilerParams(
            collective_id=0, has_side_effects=True, vmem_limit_bytes=60 * 1024 * 1024
        ),
    )(ensemble, control, weights, member_band, spread, advect, damping, innovation, obs_weight)
    total_cells = tiles * rows * ny * vl
    return out, gw[:ml, 0] / math.sqrt(total_cells)


def solution(mesh):
    in_specs = (
        P("mem", None, "tile", None),
        P("mem", "tile", None),
        P("mem"),
        P("mem"),
        P(),
        P(),
        P(),
        P(None, "tile", None),
        P("tile", None),
    )
    out_specs = (P("mem", "tile", None), P("mem"))
    return jax.shard_map(
        functools.partial(per_device, mesh.shape["mem"], mesh.shape["tile"]),
        mesh=mesh, in_specs=in_specs, out_specs=out_specs, check_vma=False,
    )
```

profile of v0, /device:TPU:0, one launch (start us, length us, event | category | flops | bytes accessed | tf_op | source)
XLA Modules:
  0.0 50.0 jit_solution(3636019307463650219)
XLA Ops:
  0.6 46.7 %shard_map.104 = (f32[2,8,256]{2,1,0:T(8,128)}, f32[8,128]{1,0:T(8,128)}) custom-call(bf16[2,256,8,256]{3,2,1,0:T(8,128)(2,1)} %ens.1, f32[2,8,256]{2,1,0:T(8,128)} %control_h.1, f32[2]{0:T(128)} %weights_h.1, s32[2]{0:T(128)} %band_h.1, f32[4]{0:T(128)} %spread_h.1, f32[2,256]{1,0:T(2,128)} %advect_h.1, f32[256]{0:T(256)} %damping_h.1, ...), custom_call_target="tpu_custom_call" | custom-call | tf_op jit(solution)/shard_map/pallas_call | solution.py:615
  47.4 1.3 %multiply_reduce_fusion = f32[2]{0:T(128)} fusion(f32[8,128]{1,0:T(8,128)} %get-tuple-element.5), kind=kLoop, calls=%fused_computation | loop fusion | flops 2 | bytes 16 | tf_op jit(solution)/shard_map/div | solution.py:637
  48.7 1.3 %copy.12 = f32[2,8,256]{2,1,0:T(8,128)} copy(f32[2,8,256]{2,1,0:T(8,128)} %get-tuple-element.8) | data formatting | bytes 32768
where the time goes:
time: 50.2 us; the launch traced here: 50 us
  Pallas kernels  46.7 us (93%)
  local copies, waits for them, and re-layouts  1.32 us (3%)
  other arithmetic  1.3 us (3%)
  between operations  0.64 us (1%)
    pallas_call x1, Pallas kernels, per_device(): pl.pallas_call(functools.partial(kernel, n, tiles, steps, ship), out_shap...  46.7 us
    unnamed x1, local copies, waits for them, and re-layouts  1.32 us
    div x1, other arithmetic, per_device(): return (out, gw[:ml, 0] / math.sqrt(total_cells))  1.3 us

commit v1 on v0

v1 whole, which is shorter than its diff:
```python
import functools
import math

import jax
import jax.numpy as jnp
from jax import lax
from jax.experimental import pallas as pl
from jax.experimental.pallas import tpu as pltpu
from jax.sharding import PartitionSpec as P

SWEEPS = 8
CHUNKS = 4
SHIPPED = 1
AFTER = 9
LAG = 1
LANES = 128
MESH = pl.DeviceIdType.MESH


def factors(n):
    a = max(d for d in range(1, n + 1) if n % d == 0 and d * d <= n)
    return a, n // a


def y_pair(f):
    ny = f.shape[-1]
    col = lax.broadcasted_iota(jnp.int32, f.shape, 1)
    north = jnp.where(col == ny - 1, 0.0, pltpu.roll(f, ny - 1, 1))
    south = jnp.where(col == 0, 0.0, pltpu.roll(f, 1, 1))
    return north, south


def sweeps(f, rates):
    rows = f.shape[0]
    for _ in range(SWEEPS):
        north, south = y_pair(f)
        east = pltpu.roll(f, rows - 1, 0)
        west = pltpu.roll(f, 1, 0)
        f = f + rates * (east + west + north + south - 4.0 * f)
    return f


def kernel(
    n, tiles, steps, ship,
    ens, control_h, weights_h, band_h, spread_h, advect_h, damping_h, innov, obs_h,
    out, gw_out,
    args, arg_sem, e_v, buf, sems,
):
    a, b = factors(n)
    control, obs, weights, band, spread, advect, damping = args
    loc, scl, proj = buf["loc"], buf["scl"], buf["proj"]
    ml, rows, ny = control.shape
    vl = ens.shape[1]
    nc = ny // LANES
    me = lax.axis_index("mem")
    t = lax.axis_index("tile")
    nxt = (t + 1) % tiles
    prv = (t + tiles - 1) % tiles
    ia = me // b
    ib = me % b
    first = (b, a)
    second = (a, b)
    fi = (ib, ia)
    gi = (ia, ib)
    size = [vl // (2 * f) for f in first]
    chunk = [k // steps for k in size]
    both_q = sum(chunk)
    lead = (0, chunk[0])
    lead1 = (0, (first[0] - 1) * chunk[0])
    lead2 = (0, (second[0] - 1) * chunk[0])
    some_first = sum(f - 1 for f in first) > 0
    some_second = sum(g - 1 for g in second) > 0
    lone = tuple(range(ship, steps))
    sent = tuple(range(ship)) if some_first else ()
    order = lone[:AFTER] + tuple(range(ship)) + lone[AFTER:]
    near = tiles // 2 <= 2 + steps
    greet = sorted({1, tiles - 1}) if near else list(range(1, tiles))
    greet = [d for d in greet if d % tiles]

    def device(q, f, g):
        return g * b + f if q == 0 else f * b + g

    def start_of(q, owner, s):
        return pl.multiple_of(q * (vl // 2) + (owner * steps + s) * chunk[q], chunk[q])

    def ahead(q, d):
        return (fi[q] + d) % first[q]

    def behind(q, d):
        return (fi[q] + first[q] - d) % first[q]

    def to_first(q, d):
        return device(q, ahead(q, d), gi[q])

    def back_first(q, d):
        return device(q, behind(q, d), gi[q])

    def to_second(q, d):
        return device(q, fi[q], (gi[q] + d) % second[q])

    def first_peers():
        return [(q, d) for q in range(2) for d in range(1, first[q])]

    def second_peers():
        return [(q, d) for q in range(2) for d in range(1, second[q])]

    def remote(kind, index, src, dst, axis, dev):
        s_sem, r_sem = sems[kind]
        return pltpu.make_async_remote_copy(
            src_ref=src, dst_ref=dst, send_sem=s_sem.at[0], recv_sem=r_sem.at[index],
            device_id={axis: dev}, device_id_type=MESH,
        )

    def arrived(kind, index, ref):
        remote(kind, index, ref, ref, "tile", nxt).wait_recv()

    def left(kind, ref):
        remote(kind, 0, ref, ref, "tile", nxt).wait_send()

    def lanes(c):
        return slice(c * LANES, (c + 1) * LANES)

    barrier = pltpu.get_barrier_semaphore()
    for q, d in first_peers():
        pl.semaphore_signal(
            barrier, inc=1, device_id={"mem": to_first(q, d)}, device_id_type=MESH
        )
    for d in greet:
        pl.semaphore_signal(
            barrier, inc=1, device_id={"tile": (t + d) % tiles}, device_id_type=MESH
        )

    def load(k, src, dst):
        return pltpu.make_async_copy(src, dst, arg_sem.at[k])

    def ens_load(k, q, owner, s, count):
        where = pl.ds(start_of(q, owner, s), count * chunk[q])
        return load(k, ens.at[:, where], e_v.at[:, where])

    early = [ens_load(0, q, ahead(q, d), 0, ship) for q, d in first_peers() if ship]
    late = [ens_load(1, q, fi[q], 0, steps) for q in range(2)]
    late += [ens_load(1, q, ahead(q, d), ship, steps - ship) for q, d in first_peers()]
    innov_load = [
        load(
            2,
            innov.at[pl.ds(start_of(q, fi[q], s), chunk[q]), :, lanes(c)],
            buf["iv"].at[pl.ds(s * both_q + lead[q], chunk[q]), c],
        )
        for s in range(steps)
        for q in range(2)
        for c in range(nc)
    ]
    arg_load = [
        load(3 + i, src, dst)
        for i, (src, dst) in enumerate((
            (control_h, control), (obs_h, obs), (weights_h, weights), (band_h, band),
            (spread_h, spread), (advect_h, advect), (damping_h, damping),
        ))
    ]
    for c in early + arg_load + innov_load + late:
        c.start()
    early_planes = ship * sum((first[q] - 1) * chunk[q] for q in range(2))

    def block1(q, d, per=1):
        return pl.ds((lead1[q] + (d - 1) * chunk[q]) * per, chunk[q] * per)

    def block2(q, d):
        return pl.ds(lead2[q] + (d - 1) * chunk[q], chunk[q])

    def own(q, s):
        return pl.ds(s * both_q + lead[q], chunk[q])

    def slot(q, d):
        return (first[0] - 1) * q + d - 1

    def ship_copy(q, s, d):
        where = block1(q, d, ml)
        return remote(
            "ship", s, buf["es"].at[s, where], buf["er"].at[s, where], "mem", to_first(q, d)
        )

    def scl_copy(q, d):
        return remote("scl", 0, scl, buf["sr"].at[slot(q, d)], "mem", to_first(q, d))

    def part_copy(q, s, d):
        where = block1(q, d)
        return remote(
            "part", s - ship, buf["to"].at[s - ship, where], buf["r1"].at[s - ship, where],
            "mem", to_first(q, d),
        )

    def swap_copy(q, s, d):
        return remote(
            "swap", s, buf["part"].at[own(q, s)], buf["r2"].at[s, block2(q, d)],
            "mem", to_second(q, d),
        )

    def grad_copy(q, s, d):
        return remote(
            "grad", s - ship, buf["grad"].at[own(q, s)], buf["gr"].at[s - ship, block1(q, d)],
            "mem", to_first(q, d),
        )

    def proj_copy(q, d):
        return remote(
            "proj", 0, buf["pp"].at[slot(q, d)], buf["pr"].at[slot(q, d)],
            "mem", back_first(q, d),
        )

    def to_both(kind, src, dst):
        return (
            remote(kind, 0, src, dst.at[0], "tile", nxt),
            remote(kind, 0, src, dst.at[1], "tile", prv),
        )

    ip, ov = buf["ip"], buf["ov"]

    def halo(s):
        where = pl.ds(s * both_q, both_q)
        return (
            remote("halo", s, ip.at[pl.ds(rows, 2), where], ip.at[pl.ds(0, 2), where], "tile", nxt),
            remote("halo", s, ip.at[pl.ds(2, 2), where], ip.at[pl.ds(rows + 2, 2), where], "tile", prv),
        )

    c_copy = to_both("control", control, buf["ch"])
    w_copy = to_both("weight", obs, buf["wh"])
    p_copy = to_both("field", scl, buf["ph"])
    o_copy = (
        remote("innov", 0, ov.at[rows], ov.at[0], "tile", nxt),
        remote("innov", 0, ov.at[1], ov.at[rows + 1], "tile", prv),
    )

    if sent:
        where = e_v.at[:, pl.ds(0, early_planes)]
        load(0, where, where).wait()
    for s in sent:
        for q, d in first_peers():
            where = pl.ds(start_of(q, ahead(q, d), s), chunk[q])
            for m in range(ml):
                e = e_v[m, where].astype(jnp.float32)
                at = (lead1[q] + (d - 1) * chunk[q]) * ml + m * chunk[q]
                for c in range(nc):
                    buf["es"][s, at : at + chunk[q], c] = e[:, :, lanes(c)]
    pl.semaphore_wait(barrier, len(greet) + a - 1 + b - 1)
    for s in sent:
        for q, d in first_peers():
            ship_copy(q, s, d).start()
    for c in arg_load[:2]:
        c.wait()
    for c in c_copy + w_copy:
        c.start()

    load(2, buf["iv"], buf["iv"]).wait()
    flat_iv = buf["iv"].reshape(steps * both_q * nc * rows, LANES)

    @pl.loop(0, steps * both_q // 8)
    def _(j):
        for c in range(nc):
            for r in range(rows):
                ov[1 + r, pl.ds(pl.multiple_of(j * 8, 8), 8), lanes(c)] = flat_iv[
                    pl.ds(j * (8 * nc * rows) + c * rows + r, 8, stride=nc * rows), :
                ]

    for c in o_copy:
        c.start()
    for c in arg_load[2:]:
        c.wait()
    coef = buf["coef"]
    sub = lax.broadcasted_iota(jnp.int32, (8, LANES), 0)
    for q in range(2):

        @pl.loop(0, size[q] // 8)
        def _(j):
            s = j // (chunk[q] // 8)
            at = pl.multiple_of(s * both_q + lead[q] + (j % (chunk[q] // 8)) * 8, 8)
            k = start_of(q, fi[q], 0) + j * 8
            for kind, value in enumerate((
                lambda i: advect[0, i], lambda i: advect[1, i], lambda i: damping[i]
            )):
                v = jnp.full((8, LANES), value(k), jnp.float32)
                for i in range(1, 8):
                    v = jnp.where(sub == i, value(k + i), v)
                coef[kind, pl.ds(at, 8)] = v

    rates = jnp.concatenate(
        [jnp.full((3 * rows, ny), spread[band[m]], jnp.float32) for m in range(ml)], axis=0
    )
    arrived("control", 0, buf["ch"])
    field = []
    for m in range(ml):
        field += [buf["ch"][0, m], control[m], buf["ch"][1, m]]
    field = sweeps(jnp.concatenate(field, axis=0), rates)
    for m in range(ml):
        center = field[(3 * m + 1) * rows : (3 * m + 2) * rows]
        loc[m] = center
        scl[m] = weights[m] * center
        proj[m] = jnp.zeros_like(center)
        for q, d in first_peers():
            buf["pp"][slot(q, d), m] = jnp.zeros_like(center)
    if sent:
        for q, d in first_peers():
            scl_copy(q, d).start()
    where = e_v.at[:, pl.ds(0, vl - early_planes)]
    load(1, where, where).wait()

    def own_sum(q, owner, s, c):
        where = pl.ds(start_of(q, owner, s), chunk[q])
        total = None
        for m in range(ml):
            term = e_v[m, where, :, lanes(c)].astype(jnp.float32) * scl[m, :, lanes(c)][None]
            total = term if total is None else total + term
        return total

    for s in lone:
        for q, d in first_peers():
            for c in range(nc):
                buf["to"][s - ship, block1(q, d), c] = own_sum(q, ahead(q, d), s, c)
            part_copy(q, s, d).start()
    for s in range(steps):
        for q in range(2):
            for c in range(nc):
                buf["part"][own(q, s), c] = own_sum(q, fi[q], s, c)
    arrived("weight", 0, buf["wh"])
    wb = buf["wb"]
    wb[0] = jnp.broadcast_to(buf["wh"][0, rows - 1 :], (8, ny))
    wb[rows + 1] = jnp.broadcast_to(buf["wh"][1, :1], (8, ny))
    for r in range(rows):
        wb[1 + r] = jnp.broadcast_to(obs[r : r + 1], (8, ny))

    def add_first(s):
        if some_first:
            if s >= ship:
                arrived("part", s - ship, buf["r1"].at[s - ship])
            else:
                arrived("ship", s, buf["er"].at[s])
        for q in range(2):
            for c in range(nc):
                total = buf["part"][own(q, s), c]
                for d in range(1, first[q]):
                    if s >= ship:
                        total = total + buf["r1"][s - ship, block1(q, d), c]
                    else:
                        for m in range(ml):
                            at = (lead1[q] + (d - 1) * chunk[q]) * ml + m * chunk[q]
                            total = total + (
                                buf["er"][s, at : at + chunk[q], c]
                                * buf["sr"][slot(q, d), m, :, lanes(c)][None]
                            )
                buf["part"][own(q, s), c] = total
            for d in range(1, second[q]):
                swap_copy(q, s, d).start()

    def add_second(s):
        if some_second:
            arrived("swap", s, buf["r2"].at[s])
        rows_of = lambda planes: planes * nc * rows
        flat = buf["part"].reshape(rows_of(steps * both_q), LANES)
        for q in range(2):
            peers = [
                buf["r2"].at[s, block2(q, d)].reshape(rows_of(chunk[q]), LANES)
                for d in range(1, second[q])
            ]
            base = s * both_q + lead[q]

            @pl.loop(0, chunk[q] // 8)
            def _(j):
                for c in range(nc):
                    for r in range(rows):
                        at = j * rows_of(8) + c * rows + r
                        total = flat[pl.ds(rows_of(base) + at, 8, stride=nc * rows), :]
                        for p in peers:
                            total = total + p[pl.ds(at, 8, stride=nc * rows), :]
                        ip[2 + r, pl.ds(pl.multiple_of(base + j * 8, 8), 8), lanes(c)] = total

        for c in halo(s):
            c.start()

    def adjoint(s):
        arrived("halo", s, ip.at[pl.ds(0, 4), pl.ds(s * both_q, both_q)])
        col = lax.broadcasted_iota(jnp.int32, (8, ny), 1)
        flat = buf["grad"].reshape(steps * both_q * nc * rows, LANES)

        @pl.loop(0, both_q // 8)
        def _(j):
            where = pl.ds(pl.multiple_of(s * both_q + j * 8, 8), 8)
            ax, ay, e = (jnp.concatenate([coef[k, where]] * nc, axis=1) for k in range(3))
            mid = 1.0 - 4.0 * e
            up = e - 0.5 * ax
            down = e + 0.5 * ax
            left_c = e - 0.5 * ay
            right_c = e + 0.5 * ay
            north1 = jnp.where(col == ny - 1, 0.0, left_c)
            south1 = jnp.where(col == 0, 0.0, right_c)
            north2 = jnp.where(col == ny - 1, 0.0, right_c)
            south2 = jnp.where(col == 0, 0.0, left_c)

            def turn(f):
                return pltpu.roll(f, ny - 1, 1), pltpu.roll(f, 1, 1)

            f = [ip[r, where, :] for r in range(rows + 4)]
            w = []
            for r in range(1, rows + 3):
                north, south = turn(f[r])
                d = (
                    mid * f[r] + up * f[r + 1] + down * f[r - 1]
                    + north1 * north + south1 * south
                )
                w.append(wb[r - 1] * (d - ov[r - 1, where, :]))
            for r in range(1, rows + 1):
                north, south = turn(w[r])
                g = (
                    mid * w[r] + down * w[r + 1] + up * w[r - 1]
                    + north2 * north + south2 * south
                )
                for c in range(nc):
                    at = (s * both_q + j * 8) * (nc * rows) + c * rows + r - 1
                    flat[pl.ds(at, 8, stride=nc * rows), :] = g[:, lanes(c)]

        if s >= ship:
            for q, d in first_peers():
                grad_copy(q, s, d).start()

    def project_own(s):
        for q in range(2):
            where = pl.ds(start_of(q, fi[q], s), chunk[q])
            for c in range(nc):
                g = buf["grad"][own(q, s), c]
                for m in range(ml):
                    e = e_v[m, where, :, lanes(c)].astype(jnp.float32)
                    proj[m, :, lanes(c)] += jnp.sum(e * g, axis=0)
                if s < ship:
                    for d in range(1, first[q]):
                        for m in range(ml):
                            at = (lead1[q] + (d - 1) * chunk[q]) * ml + m * chunk[q]
                            e = buf["er"][s, at : at + chunk[q], c]
                            buf["pp"][slot(q, d), m, :, lanes(c)] += jnp.sum(e * g, axis=0)

    def project_in(s):
        arrived("grad", s - ship, buf["gr"].at[s - ship])
        for q, d in first_peers():
            where = pl.ds(start_of(q, behind(q, d), s), chunk[q])
            for c in range(nc):
                g = buf["gr"][s - ship, block1(q, d), c]
                for m in range(ml):
                    e = e_v[m, where, :, lanes(c)].astype(jnp.float32)
                    proj[m, :, lanes(c)] += jnp.sum(e * g, axis=0)

    scope = jax.named_scope
    if sent:
        arrived("scl", 0, buf["sr"])
    for s in order:
        with scope(f"add_first{s}"):
            add_first(s)
    for tick in range(steps + LAG):
        if tick < steps:
            with scope(f"add_second{order[tick]}"):
                add_second(order[tick])
        if tick == LAG:
            arrived("innov", 0, ov.at[pl.ds(0, 2)])
        if tick >= LAG:
            s = order[tick - LAG]
            with scope(f"adjoint{s}"):
                adjoint(s)
            with scope(f"project_own{s}"):
                project_own(s)
            if sent and s == ship - 1:
                for q, d in first_peers():
                    proj_copy(q, d).start()
    if some_first:
        for s in lone:
            with scope(f"project_in{s}"):
                project_in(s)
    with scope("tail"):
        if sent:
            left("scl", buf["sr"])
            arrived("proj", 0, buf["pr"])
        for m in range(ml):
            total = proj[m]
            if sent:
                for q, d in first_peers():
                    total = total + buf["pr"][slot(q, d), m]
            proj[m] = total
            scl[m] = weights[m] * total
    with scope("halo_out"):
        for c in p_copy:
            c.start()
        gwr = buf["gwr"]
        row = lax.broadcasted_iota(jnp.int32, (8, LANES), 0)
        sums = jnp.zeros((8, LANES), jnp.float32)
        for m in range(ml):
            v = jnp.sum(loc[m] * proj[m], axis=0, keepdims=True)
            v = sum(v[:, lanes(c)] for c in range(nc))
            sums = jnp.where(row == m, jnp.broadcast_to(v, (8, LANES)), sums)
        gwr[t] = sums
        for d in range(1, tiles):
            remote("gw", 0, gwr.at[t], gwr.at[t], "tile", (t + d) % tiles).start()
        left("control", buf["ch"])
        left("weight", buf["wh"])
        left("innov", ov.at[pl.ds(0, 2)])
        left("halo", ip.at[pl.ds(0, 4)])
        if some_second:
            left("swap", buf["r2"])
        if some_first:
            left("part", buf["r1"])
            left("grad", buf["gr"])
        if sent:
            left("ship", buf["er"])
            left("proj", buf["pr"])
        arrived("field", 0, buf["ph"])
    with scope("sweeps"):
        field = []
        for m in range(ml):
            field += [buf["ph"][0, m], scl[m], buf["ph"][1, m]]
        field = sweeps(jnp.concatenate(field, axis=0), rates)
        for m in range(ml):
            out[m] = control[m] + field[(3 * m + 1) * rows : (3 * m + 2) * rows]
    with scope("finish"):
        if tiles > 1:
            arrived("gw", 0, gwr.at[pl.ds(0, tiles - 1)])
        total = gwr[0]
        for d in range(1, tiles):
            total = total + gwr[d]
        gw_out[...] = jnp.broadcast_to(jnp.sum(total, axis=1, keepdims=True), (8, LANES))
        left("field", buf["ph"])
        if tiles > 1:
            left("gw", gwr.at[pl.ds(0, tiles - 1)])


def per_device(
    n, tiles,
    ensemble, control, weights, member_band, spread, advect, damping, innovation, obs_weight
):
    ml, vl, rows, ny = ensemble.shape
    a, b = factors(n)
    first, second = (b, a), (a, b)
    assert rows == SWEEPS and ny % LANES == 0 and ml <= 8 and vl % (16 * b) == 0
    assert tiles > 2
    nc = ny // LANES
    size = [vl // (2 * f) for f in first]
    steps = max(d for d in range(1, CHUNKS + 1) if all(k % (8 * d) == 0 for k in size))
    ship = steps * SHIPPED // CHUNKS
    chunk = [k // steps for k in size]
    f32 = jnp.float32
    dma = pltpu.SemaphoreType.DMA
    hbm = pl.BlockSpec(memory_space=pl.ANY)
    whole = pl.BlockSpec(memory_space=pltpu.VMEM)
    field = (rows, ny)
    tile = (nc, rows, LANES)
    vmem = lambda *shape: pltpu.VMEM(shape, f32)
    links = max(sum(f - 1 for f in first), 1)
    block1 = max(sum((f - 1) * k for f, k in zip(first, chunk)), 8)
    block2 = max(sum((g - 1) * k for g, k in zip(second, chunk)), 8)
    ns, nl = max(ship, 1), max(steps - ship, 1)
    total = sum(size)
    buf = {
        "es": vmem(ns, ml * block1, *tile),
        "er": vmem(ns, ml * block1, *tile),
        "to": vmem(nl, block1, *tile),
        "r1": vmem(nl, block1, *tile),
        "part": vmem(total, *tile),
        "r2": vmem(steps, block2, *tile),
        "grad": vmem(total, *tile),
        "gr": vmem(nl, block1, *tile),
        "iv": vmem(total, *tile),
        "ip": vmem(rows + 4, total, ny),
        "ov": vmem(rows + 2, total, ny),
        "coef": vmem(3, total, LANES),
        "pp": vmem(links, ml, *field),
        "pr": vmem(links, ml, *field),
        "sr": vmem(links, ml, *field),
        "loc": vmem(ml, *field),
        "scl": vmem(ml, *field),
        "proj": vmem(ml, *field),
        "ch": vmem(2, ml, *field),
        "wh": vmem(2, *field),
        "wb": vmem(rows + 2, 8, ny),
        "ph": vmem(2, ml, *field),
        "gwr": vmem(tiles, 8, LANES),
    }
    pair = lambda k: (dma((1,)), dma((k,)))
    sems = {
        "ship": pair(ns), "scl": pair(1), "part": pair(nl), "swap": pair(steps),
        "grad": pair(nl), "proj": pair(1), "control": pair(1), "weight": pair(1),
        "innov": pair(1), "field": pair(1), "halo": pair(steps), "gw": pair(1),
    }
    args = (
        vmem(*control.shape),
        vmem(*obs_weight.shape),
        pltpu.SMEM(weights.shape, f32),
        pltpu.SMEM(member_band.shape, member_band.dtype),
        pltpu.SMEM(spread.shape, f32),
        pltpu.SMEM(advect.shape, f32),
        pltpu.SMEM(damping.shape, f32),
    )
    out, gw = pl.pallas_call(
        functools.partial(kernel, n, tiles, steps, ship),
        out_shape=(pltpu.VMEM((ml, rows, ny), f32), pltpu.VMEM((8, LANES), f32)),
        in_specs=[hbm] * 9,
        out_specs=(whole, whole),
        scratch_shapes=[args, dma((10,)), pltpu.VMEM((ml, vl) + field, ensemble.dtype), buf, sems],
        compiler_params=pltpu.CompilerParams(
            collective_id=0, has_side_effects=True, vmem_limit_bytes=63 * 1024 * 1024
        ),
    )(ensemble, control, weights, member_band, spread, advect, damping, innovation, obs_weight)
    total_cells = tiles * rows * ny * vl
    return out, gw[:ml, 0] / math.sqrt(total_cells)


def solution(mesh):
    in_specs = (
        P("mem", None, "tile", None),
        P("mem", "tile", None),
        P("mem"),
        P("mem"),
        P(),
        P(),
        P(),
        P(None, "tile", None),
        P("tile", None),
    )
    out_specs = (P("mem", "tile", None), P("mem"))
    return jax.shard_map(
        functools.partial(per_device, mesh.shape["mem"], mesh.shape["tile"]),
        mesh=mesh, in_specs=in_specs, out_specs=out_specs, check_vma=False,
    )
```

time: 50.2 us -> 47 us (0.936)
  Pallas kernels: 46.7 us -> 45 us
  local copies, waits for them, and re-layouts: 1.32 us -> 0.61 us
  other arithmetic: 1.3 us -> 0.63 us
    pallas_call x1, Pallas kernels: 46.7 us -> 45 us  [per_device(): pl.pallas_call(functools.partial(kernel, n, tiles, steps, ship), out_shap...]
    unnamed x1, local copies, waits for them, and re-layouts: 1.32 us -> 0.61 us
    div x1, other arithmetic: 1.3 us -> 0.63 us  [per_device(): return (out, gw[:ml, 0] / math.sqrt(total_cells))]
where the time goes in v1:
time: 47 us; the launch traced here: 46.9 us
  Pallas kernels  45 us (96%)
  between operations  0.64 us (1%)
  other arithmetic  0.63 us (1%)
  local copies, waits for them, and re-layouts  0.61 us (1%)
    pallas_call x1, Pallas kernels, per_device(): pl.pallas_call(functools.partial(kernel, n, tiles, steps, ship), out_shap...  45 us

profile of v1, /device:TPU:0, one launch (start us, length us, event | category | flops | bytes accessed | tf_op | source)
XLA Modules:
  0.0 46.9 jit_solution(17504253855157429085)
XLA Ops:
  0.6 45.0 %shard_map.104 = (f32[2,8,256]{2,1,0:T(8,128)S(1)}, f32[8,128]{1,0:T(8,128)S(1)}) custom-call(bf16[2,256,8,256]{3,2,1,0:T(8,128)(2,1)} %ens.1, f32[2,8,256]{2,1,0:T(8,128)} %control_h.1, f32[2]{0:T(128)} %weights_h.1, s32[2]{0:T(128)} %band_h.1, f32[4]{0:T(128)} %spread_h.1, f32[2,256]{1,0:T(2,128)} %advect_h.1, f32[256]{0:T(256)} %damping_h.1, ...), custom_call_target="tpu_custom_call" | custom-call | tf_op jit(solution)/shard_map/pallas_call | solution.py:595
  45.7 0.6 %copy.12 = f32[2,8,256]{2,1,0:T(8,128)} copy(f32[2,8,256]{2,1,0:T(8,128)S(1)} %get-tuple-element.6) | data formatting | bytes 32768
  46.3 0.6 %multiply_reduce_fusion = f32[2]{0:T(128)} fusion(f32[8,128]{1,0:T(8,128)S(1)} %get-tuple-element.5), kind=kLoop, calls=%fused_computation | loop fusion | flops 2 | bytes 16 | tf_op jit(solution)/shard_map/div | solution.py:606

commit v2 on v1

--- a/solution.py
+++ b/solution.py
@@ -520,10 +520,25 @@
         total = gwr[0]
         for d in range(1, tiles):
             total = total + gwr[d]
-        gw_out[...] = jnp.broadcast_to(jnp.sum(total, axis=1, keepdims=True), (8, LANES))
+        sums = jnp.broadcast_to(jnp.sum(total, axis=1, keepdims=True), (8, LANES))
+        row = lax.broadcasted_iota(jnp.int32, (8, LANES), 0)
+        lane = lax.broadcasted_iota(jnp.int32, (8, LANES), 1)
+        sums = jnp.sum(jnp.where(row == lane, sums, 0.0), axis=0)
+        gw_out[...] = sums[:ml] / math.sqrt(tiles * rows * ny * vl)
         left("field", buf["ph"])
         if tiles > 1:
             left("gw", gwr.at[pl.ds(0, tiles - 1)])
+
+
+def store(field, sums, out, gw, sem):
+    copies = [
+        pltpu.make_async_copy(src, dst, sem.at[i])
+        for i, (src, dst) in enumerate(((field, out), (sums, gw)))
+    ]
+    for c in copies:
+        c.start()
+    for c in copies:
+        c.wait()
 
 
 def per_device(
@@ -594,7 +609,7 @@
     )
     out, gw = pl.pallas_call(
         functools.partial(kernel, n, tiles, steps, ship),
-        out_shape=(pltpu.VMEM((ml, rows, ny), f32), pltpu.VMEM((8, LANES), f32)),
+        out_shape=(pltpu.VMEM((ml, rows, ny), f32), pltpu.VMEM((ml,), f32)),
         in_specs=[hbm] * 9,
         out_specs=(whole, whole),
         scratch_shapes=[args, dma((10,)), pltpu.VMEM((ml, vl) + field, ensemble.dtype), buf, sems],
@@ -602,8 +617,16 @@
             collective_id=0, has_side_effects=True, vmem_limit_bytes=63 * 1024 * 1024
         ),
     )(ensemble, control, weights, member_band, spread, advect, damping, innovation, obs_weight)
-    total_cells = tiles * rows * ny * vl
-    return out, gw[:ml, 0] / math.sqrt(total_cells)
+    return pl.pallas_call(
+        store,
+        out_shape=(
+            jax.ShapeDtypeStruct((ml, rows, ny), f32),
+            jax.ShapeDtypeStruct((ml,), f32),
+        ),
+        in_specs=[whole, whole],
+        out_specs=(hbm, hbm),
+        scratch_shapes=[dma((2,))],
+    )(*(pltpu.with_memory_space_constraint(x, pltpu.VMEM) for x in (out, gw)))
 
 
 def solution(mesh):

time: 47 us -> 46.4 us (0.987)
  Pallas kernels: 45 us -> 45.7 us
  other arithmetic: 0.63 us -> 0 us
  local copies, waits for them, and re-layouts: 0.61 us -> 0 us
    pallas_call x0 -> x1, Pallas kernels: none -> 0.63 us  [per_device(): pl.pallas_call(store, out_shape=(jax.ShapeDtypeStruct((ml, rows, ny), f32...]
    div x1 -> x0, other arithmetic: 0.63 us -> none  [per_device(): return (out, gw[:ml, 0] / math.sqrt(total_cells))]
    unnamed x1 -> x0, local copies, waits for them, and re-layouts: 0.61 us -> none
where the time goes in v2:
time: 46.4 us; the launch traced here: 46.3 us
  Pallas kernels  45.7 us (98%)
  between operations  0.64 us (1%)
    pallas_call x1, Pallas kernels, per_device(): pl.pallas_call(functools.partial(kernel, n, tiles, steps, ship), out_shap...  45 us

profile of v2, /device:TPU:0, one launch (start us, length us, event | category | flops | bytes accessed | tf_op | source)
XLA Modules:
  0.0 46.3 jit_solution(3092717055807060830)
XLA Ops:
  0.6 45.0 %shard_map.104 = (f32[2,8,256]{2,1,0:T(8,128)S(1)}, f32[2]{0:T(128)S(1)}) custom-call(bf16[2,256,8,256]{3,2,1,0:T(8,128)(2,1)} %ens.1, f32[2,8,256]{2,1,0:T(8,128)} %control_h.1, f32[2]{0:T(128)} %weights_h.1, s32[2]{0:T(128)} %band_h.1, f32[4]{0:T(128)} %spread_h.1, f32[2,256]{1,0:T(2,128)} %advect_h.1, f32[256]{0:T(256)} %damping_h.1, ...), custom_call_target="tpu_custom_call" | custom-call | tf_op jit(solution)/shard_map/pallas_call | solution.py:610
  45.7 0.6 %shard_map.105 = (f32[2,8,256]{2,1,0:T(8,128)}, f32[2]{0:T(128)}) custom-call(f32[2,8,256]{2,1,0:T(8,128)S(1)} %get-tuple-element.4.field, f32[2]{0:T(128)S(1)} %get-tuple-element.5.sums), custom_call_target="tpu_custom_call" | custom-call | tf_op jit(solution)/shard_map/pallas_call | solution.py:620

commit v3 on v2

--- a/solution.py
+++ b/solution.py
@@ -105,30 +105,16 @@
         return [(q, d) for q in range(2) for d in range(1, second[q])]
 
     def remote(kind, index, src, dst, axis, dev):
-        s_sem, r_sem = sems[kind]
         return pltpu.make_async_remote_copy(
-            src_ref=src, dst_ref=dst, send_sem=s_sem.at[0], recv_sem=r_sem.at[index],
+            src_ref=src, dst_ref=dst, send_sem=sems["sent"].at[0], recv_sem=sems[kind].at[index],
             device_id={axis: dev}, device_id_type=MESH,
         )
 
     def arrived(kind, index, ref):
         remote(kind, index, ref, ref, "tile", nxt).wait_recv()
 
-    def left(kind, ref):
-        remote(kind, 0, ref, ref, "tile", nxt).wait_send()
-
     def lanes(c):
         return slice(c * LANES, (c + 1) * LANES)
-
-    barrier = pltpu.get_barrier_semaphore()
-    for q, d in first_peers():
-        pl.semaphore_signal(
-            barrier, inc=1, device_id={"mem": to_first(q, d)}, device_id_type=MESH
-        )
-    for d in greet:
-        pl.semaphore_signal(
-            barrier, inc=1, device_id={"tile": (t + d) % tiles}, device_id_type=MESH
-        )
 
     def load(k, src, dst):
         return pltpu.make_async_copy(src, dst, arg_sem.at[k])
@@ -157,7 +143,18 @@
             (spread_h, spread), (advect_h, advect), (damping_h, damping),
         ))
     ]
-    for c in early + arg_load + innov_load + late:
+    for c in early:
+        c.start()
+    barrier = pltpu.get_barrier_semaphore()
+    for q, d in first_peers():
+        pl.semaphore_signal(
+            barrier, inc=1, device_id={"mem": to_first(q, d)}, device_id_type=MESH
+        )
+    for d in greet:
+        pl.semaphore_signal(
+            barrier, inc=1, device_id={"tile": (t + d) % tiles}, device_id_type=MESH
+        )
+    for c in arg_load + innov_load + late:
         c.start()
     early_planes = ship * sum((first[q] - 1) * chunk[q] for q in range(2))
 
@@ -224,7 +221,8 @@
 
     c_copy = to_both("control", control, buf["ch"])
     w_copy = to_both("weight", obs, buf["wh"])
-    p_copy = to_both("field", scl, buf["ph"])
+    last = buf["last"]
+    p_copy = to_both("field", last, buf["ph"])
     o_copy = (
         remote("innov", 0, ov.at[rows], ov.at[0], "tile", nxt),
         remote("innov", 0, ov.at[1], ov.at[rows + 1], "tile", prv),
@@ -472,7 +470,6 @@
                 project_in(s)
     with scope("tail"):
         if sent:
-            left("scl", buf["sr"])
             arrived("proj", 0, buf["pr"])
         for m in range(ml):
             total = proj[m]
@@ -480,37 +477,21 @@
                 for q, d in first_peers():
                     total = total + buf["pr"][slot(q, d), m]
             proj[m] = total
-            scl[m] = weights[m] * total
+            last[m] = weights[m] * total
     with scope("halo_out"):
         for c in p_copy:
             c.start()
         gwr = buf["gwr"]
-        row = lax.broadcasted_iota(jnp.int32, (8, LANES), 0)
-        sums = jnp.zeros((8, LANES), jnp.float32)
         for m in range(ml):
             v = jnp.sum(loc[m] * proj[m], axis=0, keepdims=True)
-            v = sum(v[:, lanes(c)] for c in range(nc))
-            sums = jnp.where(row == m, jnp.broadcast_to(v, (8, LANES)), sums)
-        gwr[t] = sums
+            gwr[t, m : m + 1] = sum(v[:, lanes(c)] for c in range(nc))
         for d in range(1, tiles):
             remote("gw", 0, gwr.at[t], gwr.at[t], "tile", (t + d) % tiles).start()
-        left("control", buf["ch"])
-        left("weight", buf["wh"])
-        left("innov", ov.at[pl.ds(0, 2)])
-        left("halo", ip.at[pl.ds(0, 4)])
-        if some_second:
-            left("swap", buf["r2"])
-        if some_first:
-            left("part", buf["r1"])
-            left("grad", buf["gr"])
-        if sent:
-            left("ship", buf["er"])
-            left("proj", buf["pr"])
         arrived("field", 0, buf["ph"])
     with scope("sweeps"):
         field = []
         for m in range(ml):
-            field += [buf["ph"][0, m], scl[m], buf["ph"][1, m]]
+            field += [buf["ph"][0, m], last[m], buf["ph"][1, m]]
         field = sweeps(jnp.concatenate(field, axis=0), rates)
         for m in range(ml):
             out[m] = control[m] + field[(3 * m + 1) * rows : (3 * m + 2) * rows]
@@ -520,14 +501,12 @@
         total = gwr[0]
         for d in range(1, tiles):
             total = total + gwr[d]
-        sums = jnp.broadcast_to(jnp.sum(total, axis=1, keepdims=True), (8, LANES))
-        row = lax.broadcasted_iota(jnp.int32, (8, LANES), 0)
-        lane = lax.broadcasted_iota(jnp.int32, (8, LANES), 1)
-        sums = jnp.sum(jnp.where(row == lane, sums, 0.0), axis=0)
+        total = jnp.broadcast_to(jnp.sum(total, axis=1, keepdims=True), (ml, LANES))
+        row = lax.broadcasted_iota(jnp.int32, (ml, LANES), 0)
+        lane = lax.broadcasted_iota(jnp.int32, (ml, LANES), 1)
+        sums = jnp.sum(jnp.where(row == lane, total, 0.0), axis=0)
         gw_out[...] = sums[:ml] / math.sqrt(tiles * rows * ny * vl)
-        left("field", buf["ph"])
-        if tiles > 1:
-            left("gw", gwr.at[pl.ds(0, tiles - 1)])
+        remote("gw", 0, buf["all"], buf["all"], "tile", nxt).wait_send()
 
 
 def store(field, sums, out, gw, sem):
@@ -567,6 +546,12 @@
     block2 = max(sum((g - 1) * k for g, k in zip(second, chunk)), 8)
     ns, nl = max(ship, 1), max(steps - ship, 1)
     total = sum(size)
+    out1 = sum((f - 1) * k for f, k in zip(first, chunk))
+    out2 = sum((g - 1) * k for g, k in zip(second, chunk))
+    fields = 2 * (steps - ship) * out1 + steps * out2 + 4 * ml + 2
+    if ship:
+        fields += ship * ml * out1 + 2 * ml * sum(f - 1 for f in first)
+    sent_rows = fields * nc * rows + 6 * total * nc + (tiles - 1) * ml
     buf = {
         "es": vmem(ns, ml * block1, *tile),
         "er": vmem(ns, ml * block1, *tile),
@@ -590,13 +575,15 @@
         "wh": vmem(2, *field),
         "wb": vmem(rows + 2, 8, ny),
         "ph": vmem(2, ml, *field),
-        "gwr": vmem(tiles, 8, LANES),
+        "gwr": vmem(tiles, ml, LANES),
+        "last": vmem(ml, *field),
+        "all": vmem(sent_rows, LANES),
     }
-    pair = lambda k: (dma((1,)), dma((k,)))
     sems = {
-        "ship": pair(ns), "scl": pair(1), "part": pair(nl), "swap": pair(steps),
-        "grad": pair(nl), "proj": pair(1), "control": pair(1), "weight": pair(1),
-        "innov": pair(1), "field": pair(1), "halo": pair(steps), "gw": pair(1),
+        "sent": dma((1,)), "ship": dma((ns,)), "scl": dma((1,)), "part": dma((nl,)),
+        "swap": dma((steps,)), "grad": dma((nl,)), "proj": dma((1,)), "control": dma((1,)),
+        "weight": dma((1,)), "innov": dma((1,)), "field": dma((1,)), "halo": dma((steps,)),
+        "gw": dma((1,)),
     }
     args = (
         vmem(*control.shape),

time: 46.4 us -> 46.2 us (level)
  no operation moved by 1% of the time
where the time goes in v3:
time: 46.2 us; the launch traced here: 46.1 us
  Pallas kernels  45.5 us (98%)
  between operations  0.64 us (1%)
    pallas_call x1, Pallas kernels, per_device(): pl.pallas_call(functools.partial(kernel, n, tiles, steps, ship), out_shap...  44.8 us

profile of v3, /device:TPU:0, one launch (start us, length us, event | category | flops | bytes accessed | tf_op | source)
XLA Modules:
  0.0 46.1 jit_solution(7009287399840993902)
XLA Ops:
  0.6 44.8 %shard_map.104 = (f32[2,8,256]{2,1,0:T(8,128)S(1)}, f32[2]{0:T(128)S(1)}) custom-call(bf16[2,256,8,256]{3,2,1,0:T(8,128)(2,1)} %ens.1, f32[2,8,256]{2,1,0:T(8,128)} %control_h.1, f32[2]{0:T(128)} %weights_h.1, s32[2]{0:T(128)} %band_h.1, f32[4]{0:T(128)} %spread_h.1, f32[2,256]{1,0:T(2,128)} %advect_h.1, f32[256]{0:T(256)} %damping_h.1, ...), custom_call_target="tpu_custom_call" | custom-call | tf_op jit(solution)/shard_map/pallas_call | solution.py:597
  45.5 0.6 %shard_map.105 = (f32[2,8,256]{2,1,0:T(8,128)}, f32[2]{0:T(128)}) custom-call(f32[2,8,256]{2,1,0:T(8,128)S(1)} %get-tuple-element.4.field, f32[2]{0:T(128)S(1)} %get-tuple-element.5.sums), custom_call_target="tpu_custom_call" | custom-call | tf_op jit(solution)/shard_map/pallas_call | solution.py:607

commit v4 on v3

--- a/solution.py
+++ b/solution.py
@@ -13,6 +13,7 @@
 SHIPPED = 1
 AFTER = 9
 LAG = 1
+EXTRA = 4
 LANES = 128
 MESH = pl.DeviceIdType.MESH
 
@@ -41,7 +42,7 @@
 
 
 def kernel(
-    n, tiles, steps, ship,
+    n, tiles, steps, ship, sent_rows,
     ens, control_h, weights_h, band_h, spread_h, advect_h, damping_h, innov, obs_h,
     out, gw_out,
     args, arg_sem, e_v, buf, sems,
@@ -72,6 +73,7 @@
     some_second = sum(g - 1 for g in second) > 0
     lone = tuple(range(ship, steps))
     sent = tuple(range(ship)) if some_first else ()
+    extra = EXTRA if sent and min(chunk) > EXTRA else 0
     order = lone[:AFTER] + tuple(range(ship)) + lone[AFTER:]
     near = tiles // 2 <= 2 + steps
     greet = sorted({1, tiles - 1}) if near else list(range(1, tiles))
@@ -119,13 +121,14 @@
     def load(k, src, dst):
         return pltpu.make_async_copy(src, dst, arg_sem.at[k])
 
-    def ens_load(k, q, owner, s, count):
-        where = pl.ds(start_of(q, owner, s), count * chunk[q])
+    def ens_load(k, q, owner, start, count):
+        where = pl.ds(start_of(q, owner, 0) + start, count)
         return load(k, ens.at[:, where], e_v.at[:, where])
 
-    early = [ens_load(0, q, ahead(q, d), 0, ship) for q, d in first_peers() if ship]
-    late = [ens_load(1, q, fi[q], 0, steps) for q in range(2)]
-    late += [ens_load(1, q, ahead(q, d), ship, steps - ship) for q, d in first_peers()]
+    soon = [ship * k + extra for k in chunk]
+    early = [ens_load(0, q, ahead(q, d), 0, soon[q]) for q, d in first_peers() if ship]
+    late = [ens_load(1, q, fi[q], 0, size[q]) for q in range(2)]
+    late += [ens_load(1, q, ahead(q, d), soon[q], size[q] - soon[q]) for q, d in first_peers()]
     innov_load = [
         load(
             2,
@@ -156,7 +159,7 @@
         )
     for c in arg_load + innov_load + late:
         c.start()
-    early_planes = ship * sum((first[q] - 1) * chunk[q] for q in range(2))
+    early_planes = sum((first[q] - 1) * soon[q] for q in range(2))
 
     def block1(q, d, per=1):
         return pl.ds((lead1[q] + (d - 1) * chunk[q]) * per, chunk[q] * per)
@@ -179,12 +182,31 @@
     def scl_copy(q, d):
         return remote("scl", 0, scl, buf["sr"].at[slot(q, d)], "mem", to_first(q, d))
 
-    def part_copy(q, s, d):
-        where = block1(q, d)
+    def part_copy(q, s, d, skip):
+        where = pl.ds(lead1[q] + (d - 1) * chunk[q] + skip, chunk[q] - skip)
         return remote(
-            "part", s - ship, buf["to"].at[s - ship, where], buf["r1"].at[s - ship, where],
+            "part", part_sem(q, s), buf["to"].at[s - ship, where], buf["r1"].at[s - ship, where],
             "mem", to_first(q, d),
         )
+
+    def takes(coordinate):
+        return coordinate != 0
+
+    def extra_copy(q, d):
+        where = pl.ds(((first[0] - 1) * q + d - 1) * ml * extra, ml * extra)
+        return remote(
+            "extra", q, buf["xs"].at[where], buf["xr"].at[where], "mem", to_first(q, d)
+        )
+
+    def split(copy, q, s, d, coordinate):
+        if s == ship and extra:
+            pl.when(takes(coordinate))(lambda: copy(q, s, d, extra).start())
+            pl.when(jnp.logical_not(takes(coordinate)))(lambda: copy(q, s, d, 0).start())
+        else:
+            copy(q, s, d, 0).start()
+
+    def part_sem(q, s):
+        return s - ship if s > ship or q == 0 else steps - ship
 
     def swap_copy(q, s, d):
         return remote(
@@ -192,11 +214,28 @@
             "mem", to_second(q, d),
         )
 
-    def grad_copy(q, s, d):
+    def grad_copy(q, s, d, skip):
+        count = chunk[q] - skip
         return remote(
-            "grad", s - ship, buf["grad"].at[own(q, s)], buf["gr"].at[s - ship, block1(q, d)],
+            "grad", part_sem(q, s),
+            buf["grad"].at[pl.ds(s * both_q + lead[q] + skip, count)],
+            buf["gr"].at[s - ship, pl.ds(lead1[q] + (d - 1) * chunk[q] + skip, count)],
             "mem", to_first(q, d),
         )
+
+    def arrived_split(kind, ref, some, short, full):
+        for q in range(2):
+            if first[q] > 1:
+                index = part_sem(q, ship)
+                if extra:
+                    pl.when(some(q))(
+                        lambda q=q, index=index: arrived(kind, index, ref.at[pl.ds(0, short(q))])
+                    )
+                    pl.when(jnp.logical_not(some(q)))(
+                        lambda q=q, index=index: arrived(kind, index, ref.at[pl.ds(0, full(q))])
+                    )
+                else:
+                    arrived(kind, index, ref.at[pl.ds(0, (first[q] - 1) * chunk[q])])
 
     def proj_copy(q, d):
         return remote(
@@ -239,10 +278,21 @@
                 at = (lead1[q] + (d - 1) * chunk[q]) * ml + m * chunk[q]
                 for c in range(nc):
                     buf["es"][s, at : at + chunk[q], c] = e[:, :, lanes(c)]
+    if extra:
+        for q, d in first_peers():
+            where = pl.ds(start_of(q, ahead(q, d), ship), extra)
+            for m in range(ml):
+                e = e_v[m, where].astype(jnp.float32)
+                at = (slot(q, d) * ml + m) * extra
+                for c in range(nc):
+                    buf["xs"][at : at + extra, c] = e[:, :, lanes(c)]
     pl.semaphore_wait(barrier, len(greet) + a - 1 + b - 1)
     for s in sent:
         for q, d in first_peers():
             ship_copy(q, s, d).start()
+    if extra:
+        for q, d in first_peers():
+            pl.when(takes(ahead(q, d)))(lambda q=q, d=d: extra_copy(q, d).start())
     for c in arg_load[:2]:
         c.wait()
     for c in c_copy + w_copy:
@@ -313,7 +363,7 @@
         for q, d in first_peers():
             for c in range(nc):
                 buf["to"][s - ship, block1(q, d), c] = own_sum(q, ahead(q, d), s, c)
-            part_copy(q, s, d).start()
+            split(part_copy, q, s, d, ahead(q, d))
     for s in range(steps):
         for q in range(2):
             for c in range(nc):
@@ -327,16 +377,31 @@
 
     def add_first(s):
         if some_first:
-            if s >= ship:
+            if s > ship:
                 arrived("part", s - ship, buf["r1"].at[s - ship])
+            elif s == ship:
+                arrived_split(
+                    "part", buf["r1"].at[0], lambda q: takes(fi[q]),
+                    lambda q: (first[q] - 1) * (chunk[q] - extra),
+                    lambda q: (first[q] - 1) * chunk[q],
+                )
+                for q in range(2):
+                    if extra and first[q] > 1:
+                        where = pl.ds(0, (first[q] - 1) * ml * extra)
+                        pl.when(takes(fi[q]))(
+                            lambda q=q, where=where: arrived("extra", q, buf["xr"].at[where])
+                        )
             else:
                 arrived("ship", s, buf["er"].at[s])
+        skip = extra if s == ship else 0
         for q in range(2):
+            rest = pl.ds(s * both_q + lead[q] + skip, chunk[q] - skip)
             for c in range(nc):
-                total = buf["part"][own(q, s), c]
+                total = buf["part"][rest, c]
                 for d in range(1, first[q]):
                     if s >= ship:
-                        total = total + buf["r1"][s - ship, block1(q, d), c]
+                        at = lead1[q] + (d - 1) * chunk[q]
+                        total = total + buf["r1"][s - ship, at + skip : at + chunk[q], c]
                     else:
                         for m in range(ml):
                             at = (lead1[q] + (d - 1) * chunk[q]) * ml + m * chunk[q]
@@ -344,7 +409,32 @@
                                 buf["er"][s, at : at + chunk[q], c]
                                 * buf["sr"][slot(q, d), m, :, lanes(c)][None]
                             )
-                buf["part"][own(q, s), c] = total
+                buf["part"][rest, c] = total
+            if s == ship and extra and first[q] > 1:
+                head = pl.ds(s * both_q + lead[q], extra)
+
+                @pl.when(takes(fi[q]))
+                def _(q=q, head=head):
+                    for c in range(nc):
+                        total = buf["part"][head, c]
+                        for d in range(1, first[q]):
+                            for m in range(ml):
+                                at = (slot(q, d) * ml + m) * extra
+                                total = total + (
+                                    buf["xr"][at : at + extra, c]
+                                    * buf["sr"][slot(q, d), m, :, lanes(c)][None]
+                                )
+                        buf["part"][head, c] = total
+
+                @pl.when(jnp.logical_not(takes(fi[q])))
+                def _(q=q, head=head):
+                    for c in range(nc):
+                        total = buf["part"][head, c]
+                        for d in range(1, first[q]):
+                            at = lead1[q] + (d - 1) * chunk[q]
+                            total = total + buf["r1"][0, at : at + extra, c]
+                        buf["part"][head, c] = total
+
             for d in range(1, second[q]):
                 swap_copy(q, s, d).start()
 
@@ -416,7 +506,7 @@
 
         if s >= ship:
             for q, d in first_peers():
-                grad_copy(q, s, d).start()
+                split(grad_copy, q, s, d, fi[q])
 
     def project_own(s):
         for q in range(2):
@@ -433,15 +523,45 @@
                             e = buf["er"][s, at : at + chunk[q], c]
                             buf["pp"][slot(q, d), m, :, lanes(c)] += jnp.sum(e * g, axis=0)
 
+            if s == ship and extra and first[q] > 1:
+
+                @pl.when(takes(fi[q]))
+                def _(q=q):
+                    for c in range(nc):
+                        g = buf["grad"][pl.ds(s * both_q + lead[q], extra), c]
+                        for d in range(1, first[q]):
+                            for m in range(ml):
+                                at = (slot(q, d) * ml + m) * extra
+                                e = buf["xr"][at : at + extra, c]
+                                buf["pp"][slot(q, d), m, :, lanes(c)] += jnp.sum(e * g, axis=0)
+
     def project_in(s):
-        arrived("grad", s - ship, buf["gr"].at[s - ship])
-        for q, d in first_peers():
-            where = pl.ds(start_of(q, behind(q, d), s), chunk[q])
+        if s == ship:
+            arrived_split(
+                "grad", buf["gr"].at[0], lambda q: jnp.logical_not(takes(fi[q])),
+                lambda q: (first[q] - 1) * (chunk[q] - extra),
+                lambda q: (first[q] - 1) * chunk[q] - (first[q] - 2) * extra,
+            )
+        else:
+            arrived("grad", s - ship, buf["gr"].at[s - ship])
+
+        def add(q, d, start, count):
+            where = pl.ds(start_of(q, behind(q, d), s) + start, count)
+            at = lead1[q] + (d - 1) * chunk[q] + start
             for c in range(nc):
-                g = buf["gr"][s - ship, block1(q, d), c]
+                g = buf["gr"][s - ship, at : at + count, c]
                 for m in range(ml):
                     e = e_v[m, where, :, lanes(c)].astype(jnp.float32)
                     proj[m, :, lanes(c)] += jnp.sum(e * g, axis=0)
+
+        for q, d in first_peers():
+            if s == ship and extra:
+                add(q, d, extra, chunk[q] - extra)
+                pl.when(jnp.logical_not(takes(behind(q, d))))(
+                    lambda q=q, d=d: add(q, d, 0, extra)
+                )
+            else:
+                add(q, d, 0, chunk[q])
 
     scope = jax.named_scope
     if sent:
@@ -506,7 +626,25 @@
         lane = lax.broadcasted_iota(jnp.int32, (ml, LANES), 1)
         sums = jnp.sum(jnp.where(row == lane, total, 0.0), axis=0)
         gw_out[...] = sums[:ml] / math.sqrt(tiles * rows * ny * vl)
-        remote("gw", 0, buf["all"], buf["all"], "tile", nxt).wait_send()
+        def all_left(count):
+            ref = buf["all"].at[pl.ds(0, count)]
+            remote("gw", 0, ref, ref, "tile", nxt).wait_send()
+
+        if extra:
+            for case in range(4):
+                is_first = (case % 2 == 0, case // 2 == 0)
+                change = 0
+                for q in range(2):
+                    if first[q] > 1:
+                        out = first[q] - 1 if is_first[q] else first[q] - 2
+                        change += out * (ml - 1) * extra
+                        change -= 0 if is_first[q] else (first[q] - 1) * extra
+                here = jnp.logical_and(
+                    (fi[0] == 0) == is_first[0], (fi[1] == 0) == is_first[1]
+                )
+                pl.when(here)(functools.partial(all_left, sent_rows + change * nc * rows))
+        else:
+            all_left(sent_rows)
 
 
 def store(field, sums, out, gw, sem):
@@ -577,11 +715,13 @@
         "ph": vmem(2, ml, *field),
         "gwr": vmem(tiles, ml, LANES),
         "last": vmem(ml, *field),
-        "all": vmem(sent_rows, LANES),
+        "all": vmem(sent_rows + 2 * links * ml * EXTRA * nc * rows, LANES),
+        "xs": vmem(links * ml * EXTRA, *tile),
+        "xr": vmem(links * ml * EXTRA, *tile),
     }
     sems = {
-        "sent": dma((1,)), "ship": dma((ns,)), "scl": dma((1,)), "part": dma((nl,)),
-        "swap": dma((steps,)), "grad": dma((nl,)), "proj": dma((1,)), "control": dma((1,)),
+        "sent": dma((1,)), "ship": dma((ns,)), "scl": dma((1,)), "part": dma((nl + 1,)),
+        "swap": dma((steps,)), "grad": dma((nl + 1,)), "extra": dma((2,)), "proj": dma((1,)), "control": dma((1,)),
         "weight": dma((1,)), "innov": dma((1,)), "field": dma((1,)), "halo": dma((steps,)),
         "gw": dma((1,)),
     }
@@ -595,7 +735,7 @@
         pltpu.SMEM(damping.shape, f32),
     )
     out, gw = pl.pallas_call(
-        functools.partial(kernel, n, tiles, steps, ship),
+        functools.partial(kernel, n, tiles, steps, ship, sent_rows),
         out_shape=(pltpu.VMEM((ml, rows, ny), f32), pltpu.VMEM((ml,), f32)),
         in_specs=[hbm] * 9,
         out_specs=(whole, whole),

time: 46.2 us -> 45.7 us (0.989)
  Pallas kernels: 45.5 us -> 44.9 us
    pallas_call x1, Pallas kernels: 44.8 us -> 44.3 us  [per_device(): pl.pallas_call(functools.partial(kernel, n, tiles, steps, ship, sent_rows...]
where the time goes in v4:
time: 45.7 us; the launch traced here: 45.6 us
  Pallas kernels  44.9 us (98%)
  between operations  0.64 us (1%)
    pallas_call x1, Pallas kernels, per_device(): pl.pallas_call(functools.partial(kernel, n, tiles, steps, ship, sent_rows...  44.3 us

profile of v4, /device:TPU:0, one launch (start us, length us, event | category | flops | bytes accessed | tf_op | source)
XLA Modules:
  0.0 45.6 jit_solution(5572400385721127550)
XLA Ops:
  0.6 44.3 %shard_map.104 = (f32[2,8,256]{2,1,0:T(8,128)S(1)}, f32[2]{0:T(128)S(1)}) custom-call(bf16[2,256,8,256]{3,2,1,0:T(8,128)(2,1)} %ens.1, f32[2,8,256]{2,1,0:T(8,128)} %control_h.1, f32[2]{0:T(128)} %weights_h.1, s32[2]{0:T(128)} %band_h.1, f32[4]{0:T(128)} %spread_h.1, f32[2,256]{1,0:T(2,128)} %advect_h.1, f32[256]{0:T(256)} %damping_h.1, ...), custom_call_target="tpu_custom_call" | custom-call | tf_op jit(solution)/shard_map/pallas_call | solution.py:737
  45.0 0.6 %shard_map.105 = (f32[2,8,256]{2,1,0:T(8,128)}, f32[2]{0:T(128)}) custom-call(f32[2,8,256]{2,1,0:T(8,128)S(1)} %get-tuple-element.4.field, f32[2]{0:T(128)S(1)} %get-tuple-element.5.sums), custom_call_target="tpu_custom_call" | custom-call | tf_op jit(solution)/shard_map/pallas_call | solution.py:747

commit v5 on v4

--- a/solution.py
+++ b/solution.py
@@ -23,21 +23,27 @@
     return a, n // a
 
 
-def y_pair(f):
-    ny = f.shape[-1]
+def sweeps(f, rates):
+    rows, ny = f.shape
     col = lax.broadcasted_iota(jnp.int32, f.shape, 1)
-    north = jnp.where(col == ny - 1, 0.0, pltpu.roll(f, ny - 1, 1))
-    south = jnp.where(col == 0, 0.0, pltpu.roll(f, 1, 1))
-    return north, south
-
-
-def sweeps(f, rates):
-    rows = f.shape[0]
-    for _ in range(SWEEPS):
-        north, south = y_pair(f)
-        east = pltpu.roll(f, rows - 1, 0)
-        west = pltpu.roll(f, 1, 0)
-        f = f + rates * (east + west + north + south - 4.0 * f)
+    inside = jnp.where(col == 0, 1.0, jnp.where(col == ny - 1, 1.0, 2.0))
+    c = 1.0 - 4.0 * rates
+    one = 2.0 * c * rates
+    two = rates * rates
+    here = c * c + two * inside
+
+    def along_x(g):
+        return pltpu.roll(g, rows - 1, 0) + pltpu.roll(g, 1, 0)
+
+    def along_y(g, k):
+        return jnp.where(col < ny - k, pltpu.roll(g, ny - k, 1), 0.0) + jnp.where(
+            col >= k, pltpu.roll(g, k, 1), 0.0
+        )
+
+    for _ in range(SWEEPS // 2):
+        near = along_y(f, 1)
+        inner = one * f + two * along_x(f) + (2.0 * two) * near
+        f = here * f + one * near + two * along_y(f, 2) + along_x(inner)
     return f
 
 

time: 45.7 us -> 45.4 us (level)
  no operation moved by 1% of the time
where the time goes in v5:
time: 45.4 us; the launch traced here: 45.3 us
  Pallas kernels  44.6 us (98%)
  between operations  0.64 us (1%)
    pallas_call x1, Pallas kernels, per_device(): pl.pallas_call(functools.partial(kernel, n, tiles, steps, ship, sent_rows...  44 us

profile of v5, /device:TPU:0, one launch (start us, length us, event | category | flops | bytes accessed | tf_op | source)
XLA Modules:
  0.0 45.3 jit_solution(12807141018496342532)
XLA Ops:
  0.6 44.0 %shard_map.104 = (f32[2,8,256]{2,1,0:T(8,128)S(1)}, f32[2]{0:T(128)S(1)}) custom-call(bf16[2,256,8,256]{3,2,1,0:T(8,128)(2,1)} %ens.1, f32[2,8,256]{2,1,0:T(8,128)} %control_h.1, f32[2]{0:T(128)} %weights_h.1, s32[2]{0:T(128)} %band_h.1, f32[4]{0:T(128)} %spread_h.1, f32[2,256]{1,0:T(2,128)} %advect_h.1, f32[256]{0:T(256)} %damping_h.1, ...), custom_call_target="tpu_custom_call" | custom-call | tf_op jit(solution)/shard_map/pallas_call | solution.py:743
  44.6 0.6 %shard_map.105 = (f32[2,8,256]{2,1,0:T(8,128)}, f32[2]{0:T(128)}) custom-call(f32[2,8,256]{2,1,0:T(8,128)S(1)} %get-tuple-element.4.field, f32[2]{0:T(128)S(1)} %get-tuple-element.5.sums), custom_call_target="tpu_custom_call" | custom-call | tf_op jit(solution)/shard_map/pallas_call | solution.py:753

commit v6 on v5

--- a/solution.py
+++ b/solution.py
@@ -163,7 +163,7 @@
         pl.semaphore_signal(
             barrier, inc=1, device_id={"tile": (t + d) % tiles}, device_id_type=MESH
         )
-    for c in arg_load + innov_load + late:
+    for c in arg_load:
         c.start()
     early_planes = sum((first[q] - 1) * soon[q] for q in range(2))
 
@@ -276,6 +276,8 @@
     if sent:
         where = e_v.at[:, pl.ds(0, early_planes)]
         load(0, where, where).wait()
+    for c in innov_load + late:
+        c.start()
     for s in sent:
         for q, d in first_peers():
             where = pl.ds(start_of(q, ahead(q, d), s), chunk[q])
@@ -514,6 +516,18 @@
             for q, d in first_peers():
                 split(grad_copy, q, s, d, fi[q])
 
+    def project_peers(s):
+        for q, d in first_peers():
+            for c in range(nc):
+                g = buf["grad"][own(q, s), c]
+                for m in range(ml):
+                    at = (lead1[q] + (d - 1) * chunk[q]) * ml + m * chunk[q]
+                    e = buf["er"][s, at : at + chunk[q], c]
+                    buf["pp"][slot(q, d), m, :, lanes(c)] += jnp.sum(e * g, axis=0)
+        if s == ship - 1:
+            for q, d in first_peers():
+                proj_copy(q, d).start()
+
     def project_own(s):
         for q in range(2):
             where = pl.ds(start_of(q, fi[q], s), chunk[q])
@@ -522,12 +536,6 @@
                 for m in range(ml):
                     e = e_v[m, where, :, lanes(c)].astype(jnp.float32)
                     proj[m, :, lanes(c)] += jnp.sum(e * g, axis=0)
-                if s < ship:
-                    for d in range(1, first[q]):
-                        for m in range(ml):
-                            at = (lead1[q] + (d - 1) * chunk[q]) * ml + m * chunk[q]
-                            e = buf["er"][s, at : at + chunk[q], c]
-                            buf["pp"][slot(q, d), m, :, lanes(c)] += jnp.sum(e * g, axis=0)
 
             if s == ship and extra and first[q] > 1:
 
@@ -585,11 +593,11 @@
             s = order[tick - LAG]
             with scope(f"adjoint{s}"):
                 adjoint(s)
+            if s in sent:
+                with scope(f"project_peers{s}"):
+                    project_peers(s)
             with scope(f"project_own{s}"):
                 project_own(s)
-            if sent and s == ship - 1:
-                for q, d in first_peers():
-                    proj_copy(q, d).start()
     if some_first:
         for s in lone:
             with scope(f"project_in{s}"):

time: 45.4 us -> 45.5 us (level)
  no operation moved by 1% of the time
where the time goes in v6:
time: 45.5 us; the launch traced here: 45.3 us
  Pallas kernels  44.7 us (98%)
  between operations  0.64 us (1%)
    pallas_call x1, Pallas kernels, per_device(): pl.pallas_call(functools.partial(kernel, n, tiles, steps, ship, sent_rows...  44 us

profile of v6, /device:TPU:0, one launch (start us, length us, event | category | flops | bytes accessed | tf_op | source)
XLA Modules:
  0.0 45.3 jit_solution(14557550509884675347)
XLA Ops:
  0.6 44.0 %shard_map.104 = (f32[2,8,256]{2,1,0:T(8,128)S(1)}, f32[2]{0:T(128)S(1)}) custom-call(bf16[2,256,8,256]{3,2,1,0:T(8,128)(2,1)} %ens.1, f32[2,8,256]{2,1,0:T(8,128)} %control_h.1, f32[2]{0:T(128)} %weights_h.1, s32[2]{0:T(128)} %band_h.1, f32[4]{0:T(128)} %spread_h.1, f32[2,256]{1,0:T(2,128)} %advect_h.1, f32[256]{0:T(256)} %damping_h.1, ...), custom_call_target="tpu_custom_call" | custom-call | tf_op jit(solution)/shard_map/pallas_call | solution.py:751
  44.7 0.6 %shard_map.105 = (f32[2,8,256]{2,1,0:T(8,128)}, f32[2]{0:T(128)}) custom-call(f32[2,8,256]{2,1,0:T(8,128)S(1)} %get-tuple-element.4.field, f32[2]{0:T(128)S(1)} %get-tuple-element.5.sums), custom_call_target="tpu_custom_call" | custom-call | tf_op jit(solution)/shard_map/pallas_call | solution.py:761

commit v7 on v5

--- a/solution.py
+++ b/solution.py
@@ -54,9 +54,11 @@
     args, arg_sem, e_v, buf, sems,
 ):
     a, b = factors(n)
-    control, obs, weights, band, spread, advect, damping = args
+    both_in, weights, band, spread, advect, damping = args
+    ml = both_in.shape[0] - 1
+    control, obs = both_in.at[pl.ds(0, ml)], both_in.at[ml]
     loc, scl, proj = buf["loc"], buf["scl"], buf["proj"]
-    ml, rows, ny = control.shape
+    _, rows, ny = both_in.shape
     vl = ens.shape[1]
     nc = ny // LANES
     me = lax.axis_index("mem")
@@ -264,8 +266,7 @@
             remote("halo", s, ip.at[pl.ds(2, 2), where], ip.at[pl.ds(rows + 2, 2), where], "tile", prv),
         )
 
-    c_copy = to_both("control", control, buf["ch"])
-    w_copy = to_both("weight", obs, buf["wh"])
+    c_copy = to_both("control", both_in, buf["ch"])
     last = buf["last"]
     p_copy = to_both("field", last, buf["ph"])
     o_copy = (
@@ -301,7 +302,7 @@
             pl.when(takes(ahead(q, d)))(lambda q=q, d=d: extra_copy(q, d).start())
     for c in arg_load[:2]:
         c.wait()
-    for c in c_copy + w_copy:
+    for c in c_copy:
         c.start()
 
     load(2, buf["iv"], buf["iv"]).wait()
@@ -374,10 +375,9 @@
         for q in range(2):
             for c in range(nc):
                 buf["part"][own(q, s), c] = own_sum(q, fi[q], s, c)
-    arrived("weight", 0, buf["wh"])
     wb = buf["wb"]
-    wb[0] = jnp.broadcast_to(buf["wh"][0, rows - 1 :], (8, ny))
-    wb[rows + 1] = jnp.broadcast_to(buf["wh"][1, :1], (8, ny))
+    wb[0] = jnp.broadcast_to(buf["ch"][0, ml, rows - 1 :], (8, ny))
+    wb[rows + 1] = jnp.broadcast_to(buf["ch"][1, ml, :1], (8, ny))
     for r in range(rows):
         wb[1 + r] = jnp.broadcast_to(obs[r : r + 1], (8, ny))
 
@@ -715,8 +715,7 @@
         "loc": vmem(ml, *field),
         "scl": vmem(ml, *field),
         "proj": vmem(ml, *field),
-        "ch": vmem(2, ml, *field),
-        "wh": vmem(2, *field),
+        "ch": vmem(2, ml + 1, *field),
         "wb": vmem(rows + 2, 8, ny),
         "ph": vmem(2, ml, *field),
         "gwr": vmem(tiles, ml, LANES),
@@ -728,12 +727,11 @@
     sems = {
         "sent": dma((1,)), "ship": dma((ns,)), "scl": dma((1,)), "part": dma((nl + 1,)),
         "swap": dma((steps,)), "grad": dma((nl + 1,)), "extra": dma((2,)), "proj": dma((1,)), "control": dma((1,)),
-        "weight": dma((1,)), "innov": dma((1,)), "field": dma((1,)), "halo": dma((steps,)),
+        "innov": dma((1,)), "field": dma((1,)), "halo": dma((steps,)),
         "gw": dma((1,)),
     }
     args = (
-        vmem(*control.shape),
-        vmem(*obs_weight.shape),
+        vmem(ml + 1, *field),
         pltpu.SMEM(weights.shape, f32),
         pltpu.SMEM(member_band.shape, member_band.dtype),
         pltpu.SMEM(spread.shape, f32),

time: 45.4 us -> 45.5 us (level)
  no operation moved by 1% of the time
where the time goes in v7:
time: 45.5 us; the launch traced here: 45.4 us
  Pallas kernels  44.7 us (98%)
  between operations  0.64 us (1%)
    pallas_call x1, Pallas kernels, per_device(): pl.pallas_call(functools.partial(kernel, n, tiles, steps, ship, sent_rows...  44.1 us

profile of v7, /device:TPU:0, one launch (start us, length us, event | category | flops | bytes accessed | tf_op | source)
XLA Modules:
  0.0 45.4 jit_solution(17926285545915333639)
XLA Ops:
  0.6 44.1 %shard_map.104 = (f32[2,8,256]{2,1,0:T(8,128)S(1)}, f32[2]{0:T(128)S(1)}) custom-call(bf16[2,256,8,256]{3,2,1,0:T(8,128)(2,1)} %ens.1, f32[2,8,256]{2,1,0:T(8,128)} %control_h.1, f32[2]{0:T(128)} %weights_h.1, s32[2]{0:T(128)} %band_h.1, f32[4]{0:T(128)} %spread_h.1, f32[2,256]{1,0:T(2,128)} %advect_h.1, f32[256]{0:T(256)} %damping_h.1, ...), custom_call_target="tpu_custom_call" | custom-call | tf_op jit(solution)/shard_map/pallas_call | solution.py:741
  44.8 0.6 %shard_map.105 = (f32[2,8,256]{2,1,0:T(8,128)}, f32[2]{0:T(128)}) custom-call(f32[2,8,256]{2,1,0:T(8,128)S(1)} %get-tuple-element.4.field, f32[2]{0:T(128)S(1)} %get-tuple-element.5.sums), custom_call_target="tpu_custom_call" | custom-call | tf_op jit(solution)/shard_map/pallas_call | solution.py:751
